TPU v7x, 256 devices: a whole 4x4x8 slice. The times are simulated.
256 devices in a mesh: theta: 16 (over y, z_hi, core), phi: 16 (over z_lo, x).
Axes of the slice: x: 4, y: 4, z: 8 (z_hi: 2, z_lo: 4; z = z_hi * 4 + z_lo), core: 2. Of those that a mesh axis runs over, the one named last changes fastest.
Arguments:
- fields: float32 [8, 2, 1024, 4096], P(None, None, 'theta', 'phi'), may hold values from -6 to 6
- legendre: float32 [1024, 512, 1025], P('theta', 'phi'), may hold values from -0.0029296875 to 0.0029296875
- pair_table: int32 [512], replicated, may hold values from 0 to 511, each once
Outputs:
- coefficients: float32 [512, 2, 8, 1025], P(('phi', 'theta'))
Inputs may be any that keep to these rules, and one draw needn't show every extreme that they name: A permutation: slot s holds the orders 1024 + pair_table[s] and 2047 - pair_table[s].
All inputs are finite; a program needn't handle non-finite values.
Results may differ from a plain program's by a relative error of at most 0.0003.
Values sent between devices are 32-bit elements; how exact they have to be, the bound alone decides.
A program may use at most 64 MiB of HBM per device.

v0:
```python
import math

import jax
import jax.numpy as jnp
from jax import lax
from jax.sharding import PartitionSpec as P

LONS = 4096
DEGREES = 2048
ORDERS = 1024
LOW_ORDER = 1024
PAIR_LEN = 1025


full_precision = lax.Precision.HIGHEST


def cut_along(shard, dim, devices):
    before, after = (shard.shape[:dim], shard.shape[dim + 1 :])
    return jnp.moveaxis(shard.reshape(*before, devices, -1, *after), dim, 0)


def summed_on_arrival(shard, axis, dim):
    tiles = cut_along(shard, dim, lax.axis_size(axis))
    arrived = lax.all_to_all(tiles, axis, split_axis=0, concat_axis=0, tiled=True)
    return arrived.sum(axis=0)


def order_pairs(pairs):
    return jnp.stack([LOW_ORDER + pairs, DEGREES - 1 - pairs], axis=0)


def transform(flat, orders, longitudes):
    product = longitudes[:, None, None] * orders[None, :, :] % LONS
    angles = product.astype(jnp.float32) * (2.0 * math.pi / LONS)
    cosines = jnp.cos(angles)
    sines = -jnp.sin(angles)
    real_part = jnp.einsum("rk,kan->nar", flat, cosines, precision=full_precision)
    imag_part = jnp.einsum("rk,kan->nar", flat, sines, precision=full_precision)
    return jnp.stack([real_part, imag_part], axis=1)


def order_masks(pairs):
    columns = jnp.arange(PAIR_LEN, dtype=jnp.int32)[None, :]
    shifts = pairs[:, None]
    first = columns < ORDERS - shifts
    parity = jnp.where(first, columns % 2, (columns + shifts) % 2) == 0
    even_rows = jnp.stack([first & parity, ~first & parity], axis=1)
    odd_rows = jnp.stack([first & ~parity, ~first & ~parity], axis=1)
    return jnp.stack([even_rows, odd_rows], axis=1).astype(jnp.float32)


def on_device(fields, legendre, pair_table):
    field_count = fields.shape[0]
    lat_count = fields.shape[2]
    lon_count = fields.shape[3]
    slot_count = legendre.shape[1]
    row_count = field_count * 2 * lat_count
    phi_index = lax.axis_index("phi")
    own_pairs = lax.dynamic_slice_in_dim(pair_table, phi_index * slot_count, slot_count)
    flat = fields.reshape(row_count, lon_count)
    longitudes = phi_index * lon_count + jnp.arange(lon_count, dtype=jnp.int32)
    grouped = lax.psum_scatter(
        transform(flat, order_pairs(pair_table), longitudes), "phi", scatter_dimension=0, tiled=True
    )
    grouped = grouped.reshape(slot_count, 2, 2, field_count, 2, lat_count)
    north = grouped[:, :, :, :, 0]
    south = grouped[:, :, :, :, 1]
    variants = jnp.stack([north + south, north - south], axis=1).reshape(
        slot_count, 8 * field_count, lat_count
    )
    masks = order_masks(own_pairs)
    theta_count = lax.axis_size("theta")
    product = lax.dot_general(
        variants,
        legendre,
        (((2,), (0,)), ((0,), (1,))),
        precision=full_precision,
        preferred_element_type=jnp.float32,
    )
    product = product.reshape(
        slot_count // theta_count * lax.axis_size("theta"), 2, 2, 2, field_count, PAIR_LEN
    )
    return summed_on_arrival(
        jnp.sum(product * masks[:, :, None, :, None, :], axis=(1, 3)), "theta", 0
    )


def solution(mesh):
    placed = (P(None, None, "theta", "phi"), P("theta", "phi", None), P())
    return jax.shard_map(
        on_device,
        mesh=mesh,
        in_specs=placed,
        out_specs=P(("phi", "theta"), None, None, None),
        check_vma=False,
    )
```

profile of v0, /device:TPU:1, one launch (start us, length us, event | category | flops | bytes accessed | tf_op | source)
XLA Modules:
  0.0 226.9 jit_solution(9651328543153132772)
XLA Ops:
  6.5 0.0 copy-start
  6.5 0.0 reduce-scatter.2.cloned.1.call-start
  6.5 0.8 broadcast_add_fusion
  7.3 0.5 copy-done
  7.8 7.5 %convolution_bitcast_fusion = f32[512,1,2,1024]{3,0,2,1:T(8,128)S(1)} fusion(f32[1024,256,1]{1,0,2:T(8,128)S(1)} %bitcast.37, s32[2,512]{1,0:T(2,128)S(1)} %pad_add_fusion, s32[256]{0:T(256)S(1)} %iota_add_fusion), kind=kOutput, calls=%fused_computation.4 | convolution fusion | flops 3225157632 | bytes 5248000 | tf_op jit(solution)/shard_map/rk,kan->nar/dot_general | solution.py:39
  15.3 7.7 %convolution_bitcast_fusion.1 = f32[512,1,2,1024]{3,0,2,1:T(8,128)S(1)} fusion(f32[1024,256,1]{1,0,2:T(8,128)S(1)} %bitcast.36, s32[2,512]{1,0:T(2,128)S(1)} %pad_add_fusion, s32[256]{0:T(256)S(1)} %iota_add_fusion), kind=kOutput, calls=%fused_computation.5 | convolution fusion | flops 3224895488 | bytes 5248000 | tf_op jit(solution)/shard_map/rk,kan->nar/dot_general | solution.py:38
  23.0 4.1 %pad_maximum_fusion = f32[512,2,2,1024]{3,0,2,1:T(8,128)} fusion(f32[512,1,2,1024]{3,0,2,1:T(8,128)S(1)} %convolution_bitcast_fusion, f32[512,1,2,1024]{3,0,2,1:T(8,128)S(1)} %convolution_bitcast_fusion.1), kind=kLoop, calls=%fused_computation.3 | loop fusion | flops 2097152 | bytes 16777216 | tf_op jit(solution)/shard_map/stack | solution.py:40
  27.1 0.0 reduce-scatter.2.cloned.1.call-update
  27.1 0.8 broadcast_subtract_fusion.1
  27.9 1.4 fusion.13
  29.2 0.7 add_bitcast_fusion
  30.0 0.3 add_convert_fusion
  30.3 100.3 %reduce-scatter.2.cloned.1.call-done = f32[32,2,2,1024]{3,0,2,1:T(8,128)} async-done(((f32[512,2,2,1024]{3,0,2,1:T(8,128)}), f32[32,2,2,1024]{3,0,2,1:T(8,128)}) %reduce-scatter.2.cloned.1.call-update) | async-done | bytes 524304 | tf_op jit(solution)/shard_map/reduce_scatter | solution.py:63
  130.6 1.8 reshape.387
  132.4 1.0 fusion.25
  133.4 0.1 add_bitcast_fusion.2
  133.4 0.1 pad_maximum_fusion.1
  133.5 0.1 copy.13
  133.6 15.4 %fusion = f32[32,64,1025]{2,1,0:T(8,128)S(1)} fusion(f32[32,64,64]{2,1,0:T(8,128)S(1)} %bitcast.40, f32[64,32,1025]{2,1,0:T(8,128)} %param.4), kind=kOutput, calls=%fused_computation | convolution fusion | flops 1612185600 | bytes 17317888 | tf_op jit(solution)/shard_map/dot_general | solution.py:74
  149.0 1.7 multiply_reduce_fusion
  150.7 68.6 %all_to_all.5 = f32[16,2,2,8,1025]{4,3,2,1,0:T(8,128)S(1)} all-to-all(f32[16,2,2,8,1025]{4,3,2,1,0:T(8,128)S(1)} %bitcast.39), channel_id=1, replica_groups=mesh['theta'=16,'phi'=16] {'theta'}, dimensions={0} | all-to-all | bytes 4198400 | tf_op jit(solution)/shard_map/all_to_all | solution.py:25
  219.3 0.8 reduce_sum.19
  (3 shorter events, 0.0 us)
Async XLA Ops:
  6.5 1.2 copy-start
  6.5 124.0 %reduce-scatter.2.cloned.1.call-start = ((), (), s32[]{:S(2)}) async-start(), calls=%async_computation.2 | async-start | bytes 8912896 | tf_op jit(solution)/shard_map/reduce_scatter | solution.py:63
Sparse Core Ops, SparseCore 0:
  27.2 103.3 reduce-scatter.1
where the time goes:
time: 227 us
  waiting for transfers between devices  100 us (44%)
  blocking collectives  68.6 us (30%)
  matrix products  30.6 us (13%)
  between operations  13.5 us (6%)
  other arithmetic  11.6 us (5%)
  local copies, waits for them, and re-layouts  2.37 us (1%)
    reduce_scatter x1, waiting for transfers between devices, on_device(): lax.psum_scatter(transform(flat, order_pairs(pair_table), longitudes), 'p...  100 us
    all_to_all x1, blocking collectives, summed_on_arrival(): lax.all_to_all(tiles, axis, split_axis=0, concat_axis=0, tiled=True)  68.6 us
    dot_general x1, matrix products, on_device(): lax.dot_general(variants, legendre, (((2,), (0,)), ((0,), (1,))), precisi...  15.4 us
    dot_general x1, matrix products, transform(): jnp.einsum('rk,kan->nar', flat, cosines, precision=full_precision)  7.66 us
    dot_general x1, matrix products, transform(): imag_part = jnp.einsum('rk,kan->nar', flat, sines, precision=full_precision)  7.55 us
  transfers between devices with their start and end apart: 1, of which 1 were waited for; matrix products, arithmetic and copies ran while one was open for 1% of the time, Pallas kernels for 0%

commit v1 on v0

v1 whole, which is shorter than its diff:
```python
import math

import jax
import jax.numpy as jnp
import numpy as np
from jax import lax
from jax.sharding import PartitionSpec as P

LONS = 4096
DEGREES = 2048
ORDERS = 1024
LOW_ORDER = 1024
PAIR_LEN = 1025

HIGH = lax.Precision.HIGH


def dft_tables():
    r = np.arange(16)
    k = np.arange(256)
    twiddle = 2.0 * np.pi * np.outer(r, k) / LONS
    a = np.arange(32)
    m1 = np.concatenate([64 + a, 127 - a])
    inner = 2.0 * np.pi * (np.outer(m1, k) % 256) / 256
    outer = 2.0 * np.pi * (np.outer(r, r) % 16) / 16
    return [np.stack([np.cos(t), np.sin(t)]).astype(np.float32) for t in (outer, twiddle, inner)]


def orders_of(rows):
    outer, twiddle, inner = dft_tables()
    y = jnp.einsum("zrp,pjk->zrjk", jnp.asarray(outer), rows, precision=HIGH)
    y_re, y_im = y[0], -y[1]
    c, s = jnp.asarray(twiddle)[:, :, None, :]
    z_re = y_re * c + y_im * s
    z_im = y_im * c - y_re * s
    cos, sin = inner
    both = np.stack([np.concatenate([cos, sin], 1), np.concatenate([-sin, cos], 1)])
    z = jnp.concatenate([z_re, z_im], axis=-1)
    x = jnp.einsum("znk,rjk->nrzj", jnp.asarray(both), z, precision=HIGH)
    first = x[:32].reshape(512, 2, -1)
    second = x[32:, ::-1].reshape(512, 2, -1)
    return jnp.stack([first, second])


def order_masks(pairs):
    columns = jnp.arange(PAIR_LEN, dtype=jnp.int32)[None, :]
    shifts = pairs[:, None]
    first = columns < ORDERS - shifts
    even = jnp.where(first, columns % 2, (columns + shifts) % 2) == 0
    return first[:, None, :], even[:, None, :]


def on_device(fields, legendre, pair_table):
    phi_index = lax.axis_index("phi")
    theta = lax.axis_index("theta")
    slots = legendre.shape[1]
    own_pairs = lax.dynamic_slice_in_dim(pair_table, phi_index * slots, slots)
    rows = jnp.swapaxes(fields, 0, 1).reshape(16, 64, 256)
    rows = lax.all_to_all(rows, "phi", 0, 0, tiled=True)
    x = orders_of(rows)
    x = jnp.take(x, pair_table, axis=1).reshape(2, 16, 32, 128)
    x = jnp.swapaxes(x, 0, 1)
    x = lax.all_to_all(x, "phi", 0, 0, tiled=True)
    v = x.reshape(2, 8, 2, 32, 2, 64)
    even, odd = v[0] + v[1], v[0] - v[1]
    v = jnp.stack([even, odd])
    v = v.transpose(3, 2, 0, 4, 1, 5).reshape(32, 64, 64)
    out = lax.dot_general(v, legendre, (((2,), (0,)), ((0,), (1,))), precision=HIGH)
    out = out.reshape(32, 2, 2, 16, PAIR_LEN)
    first, even = order_masks(own_pairs)
    lower = jnp.where(even, out[:, 0, 0], out[:, 0, 1])
    upper = jnp.where(even, out[:, 1, 0], out[:, 1, 1])
    part = jnp.where(first, lower, upper).reshape(4, 2, 2, 2, 16, PAIR_LEN)
    core = theta % 2
    mine = jnp.take(part, core, axis=2)
    other = jnp.take(part, 1 - core, axis=2)
    got = lax.ppermute(other, "theta", [(i, i ^ 1) for i in range(16)])
    part = mine + got
    groups = [[y * 4 + i for y in range(4)] for i in range(4)]
    part = lax.all_to_all(part, "theta", 0, 0, axis_index_groups=groups, tiled=True).sum(axis=0)
    z = (theta // 2) % 2
    mine = jnp.take(part, z, axis=0)
    other = jnp.take(part, 1 - z, axis=0)
    got = lax.ppermute(other, "theta", [(i, i ^ 2) for i in range(16)])
    return (mine + got).reshape(2, 2, 8, PAIR_LEN)


def solution(mesh):
    placed = (P(None, None, "theta", "phi"), P("theta", "phi", None), P())
    return jax.shard_map(
        on_device,
        mesh=mesh,
        in_specs=placed,
        out_specs=P(("phi", "theta"), None, None, None),
        check_vma=False,
    )
```

time: 227 us -> 122 us (0.54)
  the two profiles are of different devices: /device:TPU:1 before, /device:TPU:32 now
where the time goes in v1:
time: 122 us
  waiting for transfers between devices  65.8 us (54%)
  starting transfers between devices  22.9 us (19%)
  matrix products  14.7 us (12%)
  local copies, waits for them, and re-layouts  11.5 us (9%)
  other arithmetic  6.77 us (6%)
    all_to_all x1, waiting for transfers between devices, on_device(): rows = lax.all_to_all(rows, 'phi', 0, 0, tiled=True)  25.6 us
    all_to_all x1, waiting for transfers between devices, on_device(): lax.all_to_all(part, 'theta', 0, 0, axis_index_groups=groups, tiled=True)  16.8 us
    all_to_all x1, waiting for transfers between devices, on_device(): x = lax.all_to_all(x, 'phi', 0, 0, tiled=True)  13.1 us
    dot_general x1, matrix products, on_device(): lax.dot_general(v, legendre, (((2,), (0,)), ((0,), (1,))), precision=HIGH)  10.9 us
    all_to_all x1, starting transfers between devices, on_device(): rows = lax.all_to_all(rows, 'phi', 0, 0, tiled=True)  8.61 us
    ppermute x1, waiting for transfers between devices, on_device(): got = lax.ppermute(other, 'theta', [(i, i ^ 2) for i in range(16)])  7.33 us
    all_to_all x1, starting transfers between devices, on_device(): x = lax.all_to_all(x, 'phi', 0, 0, tiled=True)  5.15 us
    ppermute x1, starting transfers between devices, on_device(): got = lax.ppermute(other, 'theta', [(i, i ^ 2) for i in range(16)])  4.58 us
  transfers between devices with their start and end apart: 5, of which 5 were waited for; matrix products, arithmetic and copies ran while one was open for 1% of the time, Pallas kernels for 0%

profile of v1, /device:TPU:32, one launch (start us, length us, event | category | flops | bytes accessed | tf_op | source)
XLA Modules:
  0.0 121.9 jit_solution(12681348572110822068)
XLA Ops:
  0.0 0.0 copy-start.3
  0.0 0.0 copy-start.4
  0.0 2.3 %copy.23 = f32[2,8,64,256]{3,2,1,0:T(8,128)} copy(f32[2,8,64,256]{3,2,0,1:T(8,128)} %bitcast.76) | data formatting | bytes 2097152 | tf_op jit(solution)/shard_map/transpose | solution.py:58
  2.3 0.0 copy-start.1
  2.3 0.0 copy-start.2
  2.3 8.6 %all-to-all-start = ((f32[16,64,256]{2,1,0:T(8,128)}), f32[16,64,256]{2,1,0:T(8,128)S(1)}, u32[]{:S(2)}, u32[]{:S(2)}) async-start(f32[16,64,256]{2,1,0:T(8,128)} %bitcast.3), calls=%async_computation | async-start | bytes 2097152 | tf_op jit(solution)/shard_map/all_to_all | solution.py:59
  10.9 0.0 copy-done.4
  11.0 0.1 broadcast_in_dim.64
  11.1 25.6 %all-to-all-done = f32[16,64,256]{2,1,0:T(8,128)S(1)} async-done(((f32[16,64,256]{2,1,0:T(8,128)}), f32[16,64,256]{2,1,0:T(8,128)S(1)}, u32[]{:S(2)}, u32[]{:S(2)}) %all-to-all-start) | async-done | bytes 1048608 | tf_op jit(solution)/shard_map/all_to_all | solution.py:59
  36.7 0.0 copy-done.3
  36.7 1.3 %fusion.10 = f32[2,16,64,256]{3,1,2,0:T(8,128)S(1)} fusion(f32[2,16,16,1]{2,1,3,0:T(8,128)S(1)} %copy-done.3, f32[16,64,256]{2,1,0:T(8,128)S(1)} %all-to-all-done), kind=kOutput, calls=%fused_computation.17 | convolution fusion | flops 50331648 | bytes 3147776 | tf_op jit(solution)/shard_map/zrp,pjk->zrjk/dot_general | solution.py:31
  38.0 0.0 copy-done.1
  38.0 0.0 copy-done.2
  38.0 0.3 multiply_add_fusion
  38.3 0.0 copy-start
  38.3 0.3 maximum_bitcast_fusion
  38.7 0.6 copy-done
  39.3 2.6 %fusion.4 = f32[64,16,2,64]{3,0,2,1:T(8,128)S(1)} fusion(f32[2,64,512,1]{2,1,0,3:T(8,128)S(1)} %copy-done, f32[16,64,512,1]{2,0,1,3:T(8,128)S(1)} %maximum_bitcast_fusion), kind=kOutput, calls=%fused_computation.7 | convolution fusion | flops 402653184 | bytes 2883584 | tf_op jit(solution)/shard_map/znk,rjk->nrzj/dot_general | solution.py:39
  41.8 0.1 fusion.22
  42.0 0.3 copy.27
  42.3 0.4 copy.29
  42.7 0.3 copy.26
  43.0 0.4 copy.28
  43.4 0.5 pad_maximum_fusion
  44.0 2.8 %gather_fusion = f32[512,2,2,64]{3,2,1,0:T(2,128)S(1)} fusion(f32[2,512,2,64]{3,2,1,0:T(2,128)S(1)} %pad_maximum_fusion, s32[1024]{0:T(1024)S(1)} %pad_clamp_fusion), kind=kCustom, calls=%fused_computation | custom fusion | bytes 1050624 | tf_op jit(solution)/shard_map/jit(_take)/gather | solution.py:61
  46.8 0.9 reshape.298
  47.7 0.1 fusion.13
  47.9 0.8 copy.31
  48.7 5.2 %all-to-all-start.1 = ((f32[16,2,32,128]{3,2,1,0:T(8,128)}), f32[16,2,32,128]{3,2,1,0:T(8,128)S(1)}, u32[]{:S(2)}, u32[]{:S(2)}) async-start(f32[16,2,32,128]{3,2,1,0:T(8,128)} %copy.31), calls=%async_computation.1 | async-start | bytes 1048576 | tf_op jit(solution)/shard_map/all_to_all | solution.py:63
  53.9 0.1 broadcast_subtract_fusion
  53.9 0.1 lt.65
  54.0 0.1 add.87
  54.2 0.5 iota_compare_fusion
  54.7 13.1 %all-to-all-done.1 = f32[16,2,32,128]{3,2,1,0:T(8,128)S(1)} async-done(((f32[16,2,32,128]{3,2,1,0:T(8,128)}), f32[16,2,32,128]{3,2,1,0:T(8,128)S(1)}, u32[]{:S(2)}, u32[]{:S(2)}) %all-to-all-start.1) | async-done | bytes 524320 | tf_op jit(solution)/shard_map/all_to_all | solution.py:63
  67.8 0.3 sub.37
  68.1 0.3 add.95
  68.4 0.5 maximum_bitcast_fusion.1
  69.0 0.6 copy.32
  69.6 10.9 %fusion = f32[32,64,1025]{2,1,0:T(8,128)S(1)} fusion(f32[32,64,64]{2,1,0:T(8,128)S(1)} %bitcast.73, f32[64,32,1025]{2,1,0:T(8,128)} %param.11), kind=kOutput, calls=%fused_computation.1 | convolution fusion | flops 806092800 | bytes 17317888 | tf_op jit(solution)/shard_map/dot_general | solution.py:68
  80.5 0.9 fusion.21
  81.4 1.0 select_select_fusion
  82.4 0.1 select_bitcast_fusion
  82.5 0.1 collective-permute-start
  82.6 3.0 %collective-permute-done = f32[4,2,2,16,1025]{4,3,2,1,0:T(8,128)} collective-permute-done((f32[4,2,2,16,1025]{4,3,2,1,0:T(8,128)S(1)}, f32[4,2,2,16,1025]{4,3,2,1,0:T(8,128)}, u32[]{:S(2)}, u32[]{:S(2)}) %collective-permute-start) | collective-permute-done | bytes 1049632 | tf_op jit(solution)/shard_map/ppermute | solution.py:77
  85.6 2.4 %fusion.8 = f32[4,2,2,16,1025]{4,3,2,1,0:T(8,128)} fusion(f32[4,2,2,16,1025]{4,3,2,1,0:T(8,128)} %collective-permute-done, f32[4,2,2,2,16,1025]{5,4,3,2,1,0:T(8,128)S(1)} %select_select_fusion, s32[]{:T(128)S(6)} %select_n.104, pred[]{:T(512)S(6)} %and.64), kind=kLoop, calls=%fused_computation.10 | loop fusion | flops 524800 | bytes 3148805 | tf_op jit(solution)/shard_map/add | solution.py:78
  88.0 4.5 %all-to-all-start.2 = ((f32[4,2,2,16,1025]{4,3,2,1,0:T(8,128)}), f32[4,2,2,16,1025]{4,3,2,1,0:T(8,128)S(1)}, u32[]{:S(2)}, u32[]{:S(2)}) async-start(f32[4,2,2,16,1025]{4,3,2,1,0:T(8,128)} %fusion.8), calls=%async_computation.2 | async-start | bytes 2359296 | tf_op jit(solution)/shard_map/all_to_all | solution.py:80
  92.4 16.8 %all-to-all-done.2 = f32[4,2,2,16,1025]{4,3,2,1,0:T(8,128)S(1)} async-done(((f32[4,2,2,16,1025]{4,3,2,1,0:T(8,128)}), f32[4,2,2,16,1025]{4,3,2,1,0:T(8,128)S(1)}, u32[]{:S(2)}, u32[]{:S(2)}) %all-to-all-start.2) | async-done | bytes 1049632 | tf_op jit(solution)/shard_map/all_to_all | solution.py:80
  109.2 0.1 reduce_sum.9
  109.4 4.6 %collective-permute-start.1 = (f32[2,16,1025]{2,1,0:T(8,128)S(1)}, f32[2,16,1025]{2,1,0:T(8,128)S(1)}, u32[]{:S(2)}, u32[]{:S(2)}) collective-permute-start(f32[2,16,1025]{2,1,0:T(8,128)S(1)} %select_bitcast_fusion.1), channel_id=1, source_target_pairs={{0,32},{16,48},{32,0},{48,16},{64,96},{80,112},{96,64},{112,80},{1... | collective-permute-start | bytes 393608 | tf_op jit(solution)/shard_map/ppermute | solution.py:84
  113.9 7.3 %collective-permute-done.1 = f32[2,16,1025]{2,1,0:T(8,128)S(1)} collective-permute-done((f32[2,16,1025]{2,1,0:T(8,128)S(1)}, f32[2,16,1025]{2,1,0:T(8,128)S(1)}, u32[]{:S(2)}, u32[]{:S(2)}) %collective-permute-start.1) | collective-permute-done | bytes 131232 | tf_op jit(solution)/shard_map/ppermute | solution.py:84
  121.3 0.7 fusion.16
  (7 shorter events, 0.1 us)
Async XLA Ops:
  0.0 36.7 %copy-start.3 = (f32[2,16,16,1]{2,1,3,0:T(8,128)S(1)}, f32[2,16,16,1]{2,1,3,0:T(8,128)}, u32[]{:S(2)}) copy-start(f32[2,16,16,1]{2,1,3,0:T(8,128)} %constant.162) | copy-start | bytes 6148
  0.0 10.9 %copy-start.4 = (s32[512]{0:T(512)S(1)}, s32[512]{0:T(512)}, u32[]{:S(2)}) copy-start(s32[512]{0:T(512)} %param.12) | copy-start | bytes 6148
  2.3 35.7 %copy-start.1 = (f32[16,256]{1,0:T(8,128)S(1)}, f32[16,256]{1,0:T(8,128)}, u32[]{:S(2)}) copy-start(f32[16,256]{1,0:T(8,128)} %constant.149) | copy-start | bytes 49156
  2.3 35.7 %copy-start.2 = (f32[16,256]{1,0:T(8,128)S(1)}, f32[16,256]{1,0:T(8,128)}, u32[]{:S(2)}) copy-start(f32[16,256]{1,0:T(8,128)} %constant.147) | copy-start | bytes 49156
  2.3 34.3 %all-to-all-start = ((f32[16,64,256]{2,1,0:T(8,128)}), f32[16,64,256]{2,1,0:T(8,128)S(1)}, u32[]{:S(2)}, u32[]{:S(2)}) async-start(f32[16,64,256]{2,1,0:T(8,128)} %bitcast.3), calls=%async_computation | async-start | bytes 2097152 | tf_op jit(solution)/shard_map/all_to_all | solution.py:59
  38.3 1.0 copy-start
  48.7 19.0 %all-to-all-start.1 = ((f32[16,2,32,128]{3,2,1,0:T(8,128)}), f32[16,2,32,128]{3,2,1,0:T(8,128)S(1)}, u32[]{:S(2)}, u32[]{:S(2)}) async-start(f32[16,2,32,128]{3,2,1,0:T(8,128)} %copy.31), calls=%async_computation.1 | async-start | bytes 1048576 | tf_op jit(solution)/shard_map/all_to_all | solution.py:63
  82.5 3.1 %collective-permute-start = (f32[4,2,2,16,1025]{4,3,2,1,0:T(8,128)S(1)}, f32[4,2,2,16,1025]{4,3,2,1,0:T(8,128)}, u32[]{:S(2)}, u32[]{:S(2)}) collective-permute-start(f32[4,2,2,16,1025]{4,3,2,1,0:T(8,128)S(1)} %select_bitcast_fusion), channel_id=1, source_target_pairs={{0,16},{16,0},{32,48},{48,32},{64,80},{80,64},{96,112},{112,96},{1... | collective-permute-start | bytes 3148808 | tf_op jit(solution)/shard_map/ppermute | solution.py:77
  88.0 21.3 %all-to-all-start.2 = ((f32[4,2,2,16,1025]{4,3,2,1,0:T(8,128)}), f32[4,2,2,16,1025]{4,3,2,1,0:T(8,128)S(1)}, u32[]{:S(2)}, u32[]{:S(2)}) async-start(f32[4,2,2,16,1025]{4,3,2,1,0:T(8,128)} %fusion.8), calls=%async_computation.2 | async-start | bytes 2359296 | tf_op jit(solution)/shard_map/all_to_all | solution.py:80
  109.4 11.9 %collective-permute-start.1 = (f32[2,16,1025]{2,1,0:T(8,128)S(1)}, f32[2,16,1025]{2,1,0:T(8,128)S(1)}, u32[]{:S(2)}, u32[]{:S(2)}) collective-permute-start(f32[2,16,1025]{2,1,0:T(8,128)S(1)} %select_bitcast_fusion.1), channel_id=1, source_target_pairs={{0,32},{16,48},{32,0},{48,16},{64,96},{80,112},{96,64},{112,80},{1... | collective-permute-start | bytes 393608 | tf_op jit(solution)/shard_map/ppermute | solution.py:84

commit v2 on v1

v2 whole, which is shorter than its diff:
```python
import functools
import math

import jax
import jax.numpy as jnp
import numpy as np
from jax import lax
from jax.experimental import pallas as pl
from jax.experimental.pallas import tpu as pltpu
from jax.sharding import PartitionSpec as P

LONS = 4096
ORDERS = 1024
PAIR_LEN = 1025

MESH = pl.DeviceIdType.MESH
F32 = jnp.float32
BF16 = jnp.bfloat16


def dft_tables():
    r = np.arange(16)
    k = np.arange(256)
    twiddle = 2.0 * np.pi * np.outer(r, k) / LONS
    a = np.arange(32)
    m1 = np.concatenate([64 + a, 127 - a])
    inner = 2.0 * np.pi * (np.outer(m1, k) % 256) / 256
    cos, sin = np.cos(inner), np.sin(inner)
    both = np.concatenate([np.concatenate([cos, sin], 1), np.concatenate([-sin, cos], 1)])
    both = both.astype(np.float32)
    high = both.astype(BF16)
    low = (both - high.astype(np.float32)).astype(BF16)
    return np.stack([np.cos(twiddle), np.sin(twiddle)]).astype(np.float32), high, low


def halves(x):
    high = x.astype(BF16)
    return high, (x - high.astype(F32)).astype(BF16)


def weighted(terms):
    total = None
    for weight, value in terms:
        if abs(weight) < 1e-12:
            continue
        if abs(weight - 1.0) < 1e-12:
            total = value if total is None else total + value
        elif abs(weight + 1.0) < 1e-12:
            total = -value if total is None else total - value
        else:
            total = value * weight if total is None else total + value * weight
    return total


def sixteen_point(x):
    e = [None] + [x[j] + x[16 - j] for j in range(1, 8)]
    o = [None] + [x[j] - x[16 - j] for j in range(1, 8)]
    cos = lambda t: math.cos(math.pi * t / 8)
    sin = lambda t: math.sin(math.pi * t / 8)
    base = [x[0] + x[8], x[0] - x[8]]
    re_of, im_of = [], []
    plus_e = [e[j] + e[8 - j] for j in range(1, 4)]
    less_e = [e[j] - e[8 - j] for j in range(1, 4)]
    plus_o = [o[j] + o[8 - j] for j in range(1, 4)]
    less_o = [o[j] - o[8 - j] for j in range(1, 4)]
    for r in range(9):
        fold_e, fold_o = (less_e, plus_o) if r % 2 else (plus_e, less_o)
        re_terms = [(1.0, base[r % 2])] + [(cos(j * r), fold_e[j - 1]) for j in (1, 2, 3)]
        im_terms = [(-sin(j * r), fold_o[j - 1]) for j in (1, 2, 3)]
        if r % 2:
            im_terms.append((-sin(4 * r), o[4]))
        else:
            re_terms.append((cos(4 * r), e[4]))
        re_of.append(weighted(re_terms))
        im_of.append(weighted(im_terms))
    return re_of, im_of


def dot(a, b):
    return lax.dot_general(a, b, (((1,), (0,)), ((), ())), preferred_element_type=F32)


def dot_rows(a, b):
    return lax.dot_general(a, b, (((1,), (1,)), ((), ())), preferred_element_type=F32)


def kernel(
    fields, legendre, pairs, pair_scalars, twiddle, inner_high, inner_low, out,
    staged, weights, rows, z_high, z_low, a_high, a_low, chosen, ordered, arrived,
    part, from_core, ring_in, near_in, joined, joined_in, whole, from_far,
    leg_sem, s1, r1, s2, r2, sa, ra, sb, rb, sc, rc, sz, rz,
):
    theta = lax.axis_index("theta")
    phi = lax.axis_index("phi")
    z, x = phi // 4, phi % 4
    y, far, core = theta // 4, (theta // 2) % 2, theta % 2
    core_mate = theta + 1 - 2 * core
    far_mate = theta + 2 - 4 * far
    up = ((y + 1) % 4) * 4 + theta % 4
    down = ((y + 3) % 4) * 4 + theta % 4

    loads = [
        pltpu.make_async_copy(legendre.at[pl.ds(16 * c, 16)], staged.at[pl.ds(16 * c, 16)], leg_sem.at[c])
        for c in range(4)
    ]
    for load in loads:
        load.start()

    z_order = [(z + 2) % 4, 3 - z, z + 1 - 2 * (z % 2), z]
    partners = []
    for step, other_z in enumerate(z_order):
        for dx in range(4):
            if step == 3 and dx == 0:
                continue
            partners.append(other_z * 4 + (x + dx) % 4)

    barrier = pltpu.get_barrier_semaphore()
    for partner in partners:
        pl.semaphore_signal(barrier, inc=1, device_id=(theta, partner), device_id_type=MESH)
    for partner in (core_mate, far_mate, up, down):
        pl.semaphore_signal(barrier, inc=1, device_id=(partner, phi), device_id_type=MESH)
    pl.semaphore_wait(barrier, 19)

    def send(src, dst, send_sem, recv_sem, device):
        copy = pltpu.make_async_remote_copy(
            src_ref=src, dst_ref=dst, send_sem=send_sem, recv_sem=recv_sem, device_id=device, device_id_type=MESH
        )
        return copy

    first_sends = []
    for n, partner in enumerate(partners):
        copy = send(fields.at[partner % 8, partner // 8], rows.at[phi], s1.at[n], r1.at[phi], (theta, partner))
        copy.start()
        first_sends.append(copy)
    rows[phi] = fields[phi % 8, phi // 8]

    spread = jnp.broadcast_to(pairs[...].astype(F32), (128, 512))
    lane = lax.broadcasted_iota(jnp.int32, (128, 128), 1)
    for block in range(4):
        own = jnp.transpose(spread[:, 128 * block : 128 * block + 128])
        for tile in range(4):
            code = (16 * (lane % 32) + (4 * tile + lane // 32)).astype(F32)
            chosen[128 * block : 128 * block + 128, 128 * tile : 128 * tile + 128] = jnp.where(
                own == code, 1.0, 0.0
            ).astype(BF16)

    for load in loads:
        load.wait()

    def prepare(n, carry):
        lat, slot = 16 * (n // 4), 8 * (n % 4)
        for tile in range(9):
            lanes = slice(128 * tile, min(128 * tile + 128, PAIR_LEN))
            block = staged[pl.ds(lat, 16), pl.ds(slot, 8), lanes]
            high, low = halves(jnp.transpose(block, (1, 0, 2)))
            weights[pl.ds(slot, 8), pl.ds(lat, 16), lanes] = high
            weights[pl.ds(slot, 8), pl.ds(64 + lat, 16), lanes] = high
            weights[pl.ds(slot, 8), pl.ds(128 + lat, 16), lanes] = low
        return carry

    lax.fori_loop(0, 16, prepare, 0)

    for partner in partners:
        send(rows.at[partner], rows.at[partner], s1.at[0], r1.at[partner], (theta, partner)).wait_recv()

    def outer(n, carry):
        lat = 16 * (n // 2)
        lanes = pl.ds(pl.multiple_of(128 * (n % 2), 128), 128)
        upper = pl.ds(pl.multiple_of(256 + 128 * (n % 2), 128), 128)
        re_of, im_of = sixteen_point([rows[p, pl.ds(lat, 16), lanes] for p in range(16)])
        for r in range(16):
            re = re_of[min(r, 16 - r)]
            im = im_of[min(r, 16 - r)]
            c = twiddle[0, r : r + 1, lanes]
            s = twiddle[1, r : r + 1, lanes]
            if im is None:
                z_re, z_im = re * c, -(re * s)
            elif r <= 8:
                z_re, z_im = re * c + im * s, im * c - re * s
            else:
                z_re, z_im = re * c - im * s, -(im * c + re * s)
            for value, at in ((z_re, lanes), (z_im, upper)):
                high, low = halves(value)
                z_high[r, pl.ds(lat, 16), at] = high
                z_low[r, pl.ds(lat, 16), at] = low
        return carry

    lax.fori_loop(0, 8, outer, 0)

    def inner(r, carry):
        high, low = z_high[r], z_low[r]
        both = dot_rows(inner_high[...], high) + dot_rows(inner_high[...], low) + dot_rows(inner_low[...], high)
        for kind, at in ((0, r), (1, 15 - r)):
            value = jnp.concatenate([both[32 * kind : 32 * kind + 32], both[64 + 32 * kind : 96 + 32 * kind]], axis=1)
            high_value, low_value = halves(value)
            lanes = slice(128 * kind, 128 * kind + 128)
            spot = pl.ds(pl.multiple_of(32 * at, 32), 32)
            a_high[spot, lanes] = high_value
            a_low[spot, lanes] = low_value
        return carry

    lax.fori_loop(0, 16, inner, 0)

    second_sends = []
    for step, other_z in enumerate(z_order):
        at = pl.ds(pl.multiple_of(128 * other_z, 128), 128)
        picks = chosen[at, :]
        value = dot(picks, a_high[...]) + dot(picks, a_low[...])
        ordered[0, at, :] = value[:, :128]
        ordered[1, at, :] = value[:, 128:]
        for dx in range(4):
            if step == 3 and dx == 0:
                continue
            n = 4 * step + dx - (1 if step == 3 else 0)
            partner = partners[n]
            copy = send(
                ordered.at[:, pl.ds(pl.multiple_of(32 * partner, 32), 32), :],
                arrived.at[:, pl.ds(pl.multiple_of(32 * phi, 32), 32), :],
                s2.at[n],
                r2.at[phi],
                (theta, partner),
            )
            copy.start()
            second_sends.append(copy)
    mine = pl.ds(pl.multiple_of(32 * phi, 32), 32)
    arrived[:, mine, :] = ordered[:, mine, :]

    for partner in partners:
        spot = arrived.at[:, pl.ds(pl.multiple_of(32 * partner, 32), 32), :]
        send(spot, spot, s2.at[0], r2.at[partner], (theta, partner)).wait_recv()

    column = lax.broadcasted_iota(jnp.int32, (8, PAIR_LEN), 1)

    def project(slot, at):
        rows_of = []
        for kind in range(2):
            both = arrived[kind, pl.ds(slot, 16, stride=32), :]
            rows_of += [both[:8] + both[8:], both[:8] - both[8:]]
        value = jnp.concatenate(rows_of, axis=0)
        value = jnp.concatenate([value[:, :64], value[:, 64:]], axis=0)
        high = value.astype(BF16).astype(F32)
        left = jnp.concatenate([high, value - high, high], axis=1).astype(BF16)
        product = dot(left, weights[slot])
        pair = pair_scalars[32 * phi + slot]
        is_first = column < ORDERS - pair
        is_even = (column + jnp.where(is_first, 0, pair)) % 2 == 0
        for half in range(2):
            four = [product[32 * half + 8 * n : 32 * half + 8 * n + 8] for n in range(4)]
            lower = jnp.where(is_even, four[0], four[1])
            upper = jnp.where(is_even, four[2], four[3])
            part[at, 8 * half : 8 * half + 8, :] = jnp.where(is_first, lower, upper)

    def project_half(e, of_core):
        def body(n, carry):
            project(8 * (n // 2) + 4 * (n % 2) + 2 * of_core + e, 16 * e + 8 * of_core + n)
            return carry

        lax.fori_loop(0, 8, body, 0)

    core_sends, ring_sends = [], []
    for e in range(2):
        project_half(e, 1 - core)
        copy = send(
            part.at[pl.ds(16 * e + 8 * (1 - core), 8)], from_core.at[e], sa.at[e], ra.at[e], (core_mate, phi)
        )
        copy.start()
        core_sends.append(copy)
        project_half(e, core)

    def own(e, to_y, half):
        return 16 * e + 8 * core + 2 * to_y + half

    y_up, y_down, y_far = (y + 1) % 4, (y + 3) % 4, (y + 2) % 4
    near_sends = []
    for e in range(2):
        core_sends[e].wait_recv()
        mine_at = pl.ds(16 * e + 8 * core, 8)
        part[mine_at] = part[mine_at] + from_core[e]
        for n, (src, dst, device) in enumerate((
            (own(e, y_far, 0), ring_in.at[e, 0], up),
            (own(e, y_far, 1), ring_in.at[e, 1], down),
            (own(e, y_up, 1), near_in.at[e, 0], up),
            (own(e, y_down, 0), near_in.at[e, 1], down),
        )):
            copy = send(part.at[src], dst, sb.at[e, n], rb.at[e, n], (device, phi))
            copy.start()
            near_sends.append(copy)

    joined_sends = []
    for e in range(2):
        for n, (src, device) in enumerate(((own(e, y_up, 0), up), (own(e, y_down, 1), down))):
            near_sends[4 * e + n].wait_recv()
            joined[e, n] = part[src] + ring_in[e, n]
            copy = send(joined.at[e, n], joined_in.at[e, n], sc.at[e, n], rc.at[e, n], (device, phi))
            copy.start()
            joined_sends.append(copy)

    far_sends = []
    for e in range(2):
        near_sends[4 * e + 2].wait_recv()
        near_sends[4 * e + 3].wait_recv()
        joined_sends[2 * e].wait_recv()
        joined_sends[2 * e + 1].wait_recv()
        whole[e, 0] = part[own(e, y, 0)] + joined_in[e, 0] + near_in[e, 1]
        whole[e, 1] = part[own(e, y, 1)] + joined_in[e, 1] + near_in[e, 0]
        copy = send(whole.at[e, 1 - far], from_far.at[e], sz.at[e], rz.at[e], (far_mate, phi))
        copy.start()
        far_sends.append(copy)
    for e in range(2):
        far_sends[e].wait_recv()
        out[e] = whole[e, far] + from_far[e]

    for copy in first_sends + second_sends + core_sends + near_sends + joined_sends + far_sends:
        copy.wait_send()


def on_device(fields, legendre, pair_table):
    twiddle, inner_high, inner_low = dft_tables()
    vmem = pl.BlockSpec(memory_space=pltpu.VMEM)
    dma = pltpu.SemaphoreType.DMA
    row = (16, PAIR_LEN)
    result = pl.pallas_call(
        kernel,
        out_shape=jax.ShapeDtypeStruct((2, *row), F32),
        in_specs=[
            vmem,
            pl.BlockSpec(memory_space=pl.ANY),
            vmem,
            pl.BlockSpec(memory_space=pltpu.SMEM),
            vmem,
            vmem,
            vmem,
        ],
        out_specs=vmem,
        scratch_shapes=[
            pltpu.VMEM((64, 32, PAIR_LEN), F32),
            pltpu.VMEM((32, 192, PAIR_LEN), BF16),
            pltpu.VMEM((16, 64, 256), F32),
            pltpu.VMEM((16, 64, 512), BF16),
            pltpu.VMEM((16, 64, 512), BF16),
            pltpu.VMEM((512, 256), BF16),
            pltpu.VMEM((512, 256), BF16),
            pltpu.VMEM((512, 512), BF16),
            pltpu.VMEM((2, 512, 128), F32),
            pltpu.VMEM((2, 512, 128), F32),
            pltpu.VMEM((32, *row), F32),
            pltpu.VMEM((2, 8, *row), F32),
            pltpu.VMEM((2, 2, *row), F32),
            pltpu.VMEM((2, 2, *row), F32),
            pltpu.VMEM((2, 2, *row), F32),
            pltpu.VMEM((2, 2, *row), F32),
            pltpu.VMEM((2, 2, *row), F32),
            pltpu.VMEM((2, *row), F32),
            dma((4,)),
            dma((15,)), dma((16,)),
            dma((15,)), dma((16,)),
            dma((2,)), dma((2,)),
            dma((2, 4)), dma((2, 4)),
            dma((2, 2)), dma((2, 2)),
            dma((2,)), dma((2,)),
        ],
        compiler_params=pltpu.CompilerParams(
            collective_id=0, has_side_effects=True, vmem_limit_bytes=60 * 1024 * 1024
        ),
        name="harmonics",
    )(
        fields,
        legendre,
        pair_table.reshape(1, -1),
        pair_table,
        jnp.asarray(twiddle),
        jnp.asarray(inner_high),
        jnp.asarray(inner_low),
    )
    return result.reshape(2, 2, 8, PAIR_LEN)


def solution(mesh):
    placed = (P(None, None, "theta", "phi"), P("theta", "phi", None), P())
    return jax.shard_map(
        on_device,
        mesh=mesh,
        in_specs=placed,
        out_specs=P(("phi", "theta"), None, None, None),
        check_vma=False,
    )
```

time: 122 us -> 84 us (0.69)
  the two profiles are of different devices: /device:TPU:32 before, /device:TPU:1 now
where the time goes in v2:
time: 84 us; the launch traced here: 82.5 us
  Pallas kernels  80.9 us (96%)
  local copies, waits for them, and re-layouts  1.58 us (2%)
    pallas_call x1, Pallas kernels, on_device(): pl.pallas_call(kernel, out_shape=jax.ShapeDtypeStruct((2, *row), F32), in...  80.9 us

profile of v2, /device:TPU:1, one launch (start us, length us, event | category | flops | bytes accessed | tf_op | source)
XLA Modules:
  0.0 82.5 jit_solution(7469999527932357143)
XLA Ops:
  0.0 80.9 %harmonics.1 = f32[2,16,1025]{2,1,0:T(8,128)} custom-call(f32[8,2,64,256]{3,2,1,0:T(8,128)} %fields.1, f32[64,32,1025]{2,1,0:T(8,128)} %legendre.1, s32[1,512]{1,0:T(1,128)} %bitcast.3, s32[512]{0:T(512)} %pair_scalars.1, f32[2,16,256]{2,1,0:T(8,128)} %constant.6.clone.twiddle, bf16[128,512]{1,0:T(8,128)(2,1)} %constant.7.clone.inner_high, ...), custom_call_target="tpu_custom_call" | custom-call | tf_op jit(solution)/shard_map/harmonics/pallas_call | solution.py:322
  80.9 1.6 %copy.8 = f32[2,2,8,1025]{3,2,1,0:T(8,128)} copy(f32[2,2,8,1025]{3,2,1,0:T(8,128)} %bitcast.2) | data formatting | bytes 262400

commit v3 on v2

v3 whole, which is shorter than its diff:
```python
import functools
import math

import jax
import jax.numpy as jnp
import numpy as np
from jax import lax
from jax.experimental import pallas as pl
from jax.experimental.pallas import tpu as pltpu
from jax.sharding import PartitionSpec as P

LONS = 4096
ORDERS = 1024
PAIR_LEN = 1025

MESH = pl.DeviceIdType.MESH
F32 = jnp.float32
BF16 = jnp.bfloat16


def dft_tables():
    r = np.arange(16)
    k = np.arange(256)
    twiddle = 2.0 * np.pi * np.outer(r, k) / LONS
    a = np.arange(32)
    m1 = np.concatenate([64 + a, 127 - a])
    inner = 2.0 * np.pi * (np.outer(m1, k) % 256) / 256
    cos, sin = np.cos(inner), np.sin(inner)
    both = np.stack([np.concatenate([cos, sin], 1), np.concatenate([-sin, cos], 1)])
    both = both.reshape(2, 2, 32, 512).transpose(1, 0, 2, 3).reshape(128, 512)
    both = both.astype(np.float32)
    high = both.astype(BF16)
    low = (both - high.astype(np.float32)).astype(BF16)
    return np.stack([np.cos(twiddle), np.sin(twiddle)]).astype(np.float32), high, low


def halves(x):
    high = x.astype(BF16)
    return high, (x - high.astype(F32)).astype(BF16)


def weighted(terms):
    total = None
    for weight, value in terms:
        if abs(weight) < 1e-12:
            continue
        if abs(weight - 1.0) < 1e-12:
            total = value if total is None else total + value
        elif abs(weight + 1.0) < 1e-12:
            total = -value if total is None else total - value
        else:
            total = value * weight if total is None else total + value * weight
    return total


def sixteen_point(x):
    e = [None] + [x[j] + x[16 - j] for j in range(1, 8)]
    o = [None] + [x[j] - x[16 - j] for j in range(1, 8)]
    cos = lambda t: math.cos(math.pi * t / 8)
    sin = lambda t: math.sin(math.pi * t / 8)
    base = [x[0] + x[8], x[0] - x[8]]
    re_of, im_of = [], []
    plus_e = [e[j] + e[8 - j] for j in range(1, 4)]
    less_e = [e[j] - e[8 - j] for j in range(1, 4)]
    plus_o = [o[j] + o[8 - j] for j in range(1, 4)]
    less_o = [o[j] - o[8 - j] for j in range(1, 4)]
    for r in range(9):
        fold_e, fold_o = (less_e, plus_o) if r % 2 else (plus_e, less_o)
        re_terms = [(1.0, base[r % 2])] + [(cos(j * r), fold_e[j - 1]) for j in (1, 2, 3)]
        im_terms = [(-sin(j * r), fold_o[j - 1]) for j in (1, 2, 3)]
        if r % 2:
            im_terms.append((-sin(4 * r), o[4]))
        else:
            re_terms.append((cos(4 * r), e[4]))
        re_of.append(weighted(re_terms))
        im_of.append(weighted(im_terms))
    return re_of, im_of


def dot(a, b):
    return lax.dot_general(a, b, (((1,), (0,)), ((), ())), preferred_element_type=F32)


def dot_rows(a, b):
    return lax.dot_general(a, b, (((1,), (1,)), ((), ())), preferred_element_type=F32)


def kernel(
    fields, legendre, pairs, pair_scalars, twiddle, inner_high, inner_low, out,
    staged, weights, rows, z_high, z_low, a_high, a_low, spread_pairs, chosen, ordered, arrived,
    left, part, from_core, ring_in, near_in, joined, joined_in, whole, from_far,
    leg_sem, s1, r1, s2, r2, sa, ra, sb, rb, sc, rc, sz, rz,
):
    theta = lax.axis_index("theta")
    phi = lax.axis_index("phi")
    z, x = phi // 4, phi % 4
    y, far, core = theta // 4, (theta // 2) % 2, theta % 2
    core_mate = theta + 1 - 2 * core
    far_mate = theta + 2 - 4 * far
    up = ((y + 1) % 4) * 4 + theta % 4
    down = ((y + 3) % 4) * 4 + theta % 4

    loads = [
        pltpu.make_async_copy(legendre.at[pl.ds(16 * c, 16)], staged.at[pl.ds(16 * c, 16)], leg_sem.at[c])
        for c in range(4)
    ]
    for load in loads:
        load.start()

    z_order = [(z + 2) % 4, 3 - z, z + 1 - 2 * (z % 2), z]
    partners = []
    for step, other_z in enumerate(z_order):
        for dx in range(4):
            if step == 3 and dx == 0:
                continue
            partners.append(other_z * 4 + (x + dx) % 4)

    barrier = pltpu.get_barrier_semaphore()
    for partner in partners:
        pl.semaphore_signal(barrier, inc=1, device_id=(theta, partner), device_id_type=MESH)
    for partner in (core_mate, far_mate, up, down):
        pl.semaphore_signal(barrier, inc=1, device_id=(partner, phi), device_id_type=MESH)
    pl.semaphore_wait(barrier, 19)

    def send(src, dst, send_sem, recv_sem, device):
        return pltpu.make_async_remote_copy(
            src_ref=src, dst_ref=dst, send_sem=send_sem, recv_sem=recv_sem, device_id=device, device_id_type=MESH
        )

    sent = []

    def start(*copy_args):
        copy = send(*copy_args)
        copy.start()
        sent.append(copy)
        return copy

    for h in range(2):
        lats = pl.ds(32 * h, 32)
        for n, partner in enumerate(partners):
            start(
                fields.at[partner % 8, partner // 8, lats],
                rows.at[h, phi],
                s1.at[h, n],
                r1.at[h, phi],
                (theta, partner),
            )
        rows[h, phi] = fields[phi % 8, phi // 8, lats]

    spread = jnp.broadcast_to(pairs[...].astype(F32), (128, 512))
    for block in range(4):
        at = slice(128 * block, 128 * block + 128)
        spread_pairs[at, :] = jnp.transpose(spread[:, at])
    lane = lax.broadcasted_iota(jnp.int32, (128, 128), 1)
    for e in range(2):
        for block in range(2):
            own = spread_pairs[pl.ds(256 * block + e, 128, stride=2), :]
            for tile in range(4):
                code = (16 * (lane % 32) + (4 * tile + lane // 32)).astype(F32)
                chosen[e, 128 * block : 128 * block + 128, 128 * tile : 128 * tile + 128] = jnp.where(
                    own == code, 1.0, 0.0
                ).astype(BF16)

    def prepare(n, carry):
        lat, slot = 16 * (n // 4), 8 * (n % 4)
        for tile in range(9):
            lanes = slice(128 * tile, min(128 * tile + 128, PAIR_LEN))
            block = staged[pl.ds(lat, 16), pl.ds(slot, 8), lanes]
            high, low = halves(jnp.transpose(block, (1, 0, 2)))
            weights[pl.ds(slot, 8), pl.ds(lat, 16), lanes] = high
            weights[pl.ds(slot, 8), pl.ds(64 + lat, 16), lanes] = high
            weights[pl.ds(slot, 8), pl.ds(128 + lat, 16), lanes] = low
        return carry

    def outer(h):
        def body(n, carry):
            lat = pl.multiple_of(16 * (n // 2), 16)
            lanes = pl.ds(pl.multiple_of(128 * (n % 2), 128), 128)
            upper = pl.ds(pl.multiple_of(256 + 128 * (n % 2), 128), 128)
            re_of, im_of = sixteen_point([rows[h, p, pl.ds(lat, 16), lanes] for p in range(16)])
            for r in range(16):
                re = re_of[min(r, 16 - r)]
                im = im_of[min(r, 16 - r)]
                c = twiddle[0, r : r + 1, lanes]
                s = twiddle[1, r : r + 1, lanes]
                if im is None:
                    z_re, z_im = re * c, -(re * s)
                elif r <= 8:
                    z_re, z_im = re * c + im * s, im * c - re * s
                else:
                    z_re, z_im = re * c - im * s, -(im * c + re * s)
                for value, at in ((z_re, lanes), (z_im, upper)):
                    high, low = halves(value)
                    z_high[pl.ds(32 * r + lat, 16), at] = high
                    z_low[pl.ds(32 * r + lat, 16), at] = low
            return carry

        lax.fori_loop(0, 4, body, 0)

    def inner():
        for group in range(4):
            at = slice(128 * group, 128 * group + 128)
            high, low = z_high[at, :], z_low[at, :]
            both = dot_rows(inner_high[...], high) + dot_rows(inner_high[...], low) + dot_rows(inner_low[...], high)
            for j in range(4):
                lats = slice(32 * j, 32 * j + 32)
                r = 4 * group + j
                for kind, spot in ((0, r), (1, 15 - r)):
                    value = jnp.concatenate(
                        [both[64 * kind : 64 * kind + 32, lats], both[64 * kind + 32 : 64 * kind + 64, lats]], axis=1
                    )
                    high_value, low_value = halves(value)
                    a_high[32 * spot : 32 * spot + 32, 64 * kind : 64 * kind + 64] = high_value
                    a_low[32 * spot : 32 * spot + 32, 64 * kind : 64 * kind + 64] = low_value

    def order_and_send(h):
        for e in range(2):
            picks = chosen[e]
            ordered[h, e] = dot(picks, a_high[...]) + dot(picks, a_low[...])
            for n, partner in enumerate(partners):
                start(
                    ordered.at[h, e, pl.ds(pl.multiple_of(16 * partner, 16), 16)],
                    arrived.at[h, e, pl.ds(pl.multiple_of(16 * phi, 16), 16)],
                    s2.at[h, e, n],
                    r2.at[h, e, phi],
                    (theta, partner),
                )
            mine = pl.ds(pl.multiple_of(16 * phi, 16), 16)
            arrived[h, e, mine] = ordered[h, e, mine]

    for load in loads:
        load.wait()
    lax.fori_loop(0, 8, prepare, 0)
    for h in range(2):
        for partner in partners:
            spot = rows.at[h, partner]
            send(spot, spot, s1.at[h, 0], r1.at[h, partner], (theta, partner)).wait_recv()
        outer(h)
        inner()
        order_and_send(h)
        if h == 0:
            lax.fori_loop(8, 16, prepare, 0)

    wide = lax.broadcasted_iota(jnp.int32, (64, 128), 1)
    column = lax.broadcasted_iota(jnp.int32, (8, PAIR_LEN), 1)

    def arrive(e):
        for partner in partners:
            for h in range(2):
                spot = arrived.at[h, e, pl.ds(pl.multiple_of(16 * partner, 16), 16)]
                send(spot, spot, s2.at[h, e, 0], r2.at[h, e, partner], (theta, partner)).wait_recv()

        def body(slot, carry):
            turned = []
            for h in range(2):
                both = arrived[h, e, pl.ds(slot, 16, stride=16), :]
                both = jnp.concatenate([both[:8] + both[8:], both[:8] - both[8:]], axis=0)
                turned.append(
                    jnp.concatenate(
                        [
                            both if (32 * h - 32 * (2 * kind + p)) % 128 == 0
                            else pltpu.roll(both, (32 * h - 32 * (2 * kind + p)) % 128, 1)
                            for p in range(2) for kind in range(2)
                        ],
                        axis=0,
                    )
                )
            value = jnp.where(wide < 32, turned[0], turned[1])
            high = value.astype(BF16).astype(F32)
            low = pltpu.roll(value - high, 64, 1)
            left[slot, :, 0:128] = jnp.where(wide < 64, high, low).astype(BF16)
            left[slot, :, 128:256] = high.astype(BF16)
            return carry

        lax.fori_loop(0, 16, body, 0)

    def project(e, of_core):
        def body(n, carry):
            slot = 2 * n + of_core
            number = 2 * slot + e
            product = dot(left[slot, :, 0:192], weights[number])
            pair = pair_scalars[32 * phi + number]
            is_first = column < ORDERS - pair
            is_even = (column + jnp.where(is_first, 0, pair)) % 2 == 0
            for half in range(2):
                four = [product[32 * half + 8 * m : 32 * half + 8 * m + 8] for m in range(4)]
                lower = jnp.where(is_even, four[0], four[1])
                upper = jnp.where(is_even, four[2], four[3])
                part[e, of_core, n, 8 * half : 8 * half + 8, :] = jnp.where(is_first, lower, upper)
            return carry

        lax.fori_loop(0, 8, body, 0, unroll=2)

    y_up, y_down, y_far = (y + 1) % 4, (y + 3) % 4, (y + 2) % 4

    def to_core(e):
        project(e, 1 - core)
        copy = start(part.at[e, 1 - core], from_core.at[e], sa.at[e], ra.at[e], (core_mate, phi))
        project(e, core)
        return copy

    def to_ring(e, copy):
        copy.wait_recv()
        part[e, core] = part[e, core] + from_core[e]
        return [
            start(part.at[e, core, src], dst, sb.at[e, n], rb.at[e, n], (device, phi))
            for n, (src, dst, device) in enumerate((
                (2 * y_far, ring_in.at[e, 0], up),
                (2 * y_far + 1, ring_in.at[e, 1], down),
                (2 * y_up + 1, near_in.at[e, 0], up),
                (2 * y_down, near_in.at[e, 1], down),
            ))
        ]

    def join(e, near):
        copies = []
        for n, (src, device) in enumerate(((2 * y_up, up), (2 * y_down + 1, down))):
            near[n].wait_recv()
            joined[e, n] = part[e, core, src] + ring_in[e, n]
            copies.append(start(joined.at[e, n], joined_in.at[e, n], sc.at[e, n], rc.at[e, n], (device, phi)))
        return copies

    def to_far(e, near, last):
        for copy in near[2:] + last:
            copy.wait_recv()
        whole[e, 0] = part[e, core, 2 * y] + joined_in[e, 0] + near_in[e, 1]
        whole[e, 1] = part[e, core, 2 * y + 1] + joined_in[e, 1] + near_in[e, 0]
        return start(whole.at[e, 1 - far], from_far.at[e], sz.at[e], rz.at[e], (far_mate, phi))

    arrive(0)
    near0 = to_ring(0, to_core(0))
    arrive(1)
    core1 = to_core(1)
    last0 = join(0, near0)
    near1 = to_ring(1, core1)
    far0 = to_far(0, near0, last0)
    last1 = join(1, near1)
    far1 = to_far(1, near1, last1)
    for e, copy in enumerate((far0, far1)):
        copy.wait_recv()
        out[e] = whole[e, far] + from_far[e]

    for copy in sent:
        copy.wait_send()


def on_device(fields, legendre, pair_table):
    twiddle, inner_high, inner_low = dft_tables()
    vmem = pl.BlockSpec(memory_space=pltpu.VMEM)
    dma = pltpu.SemaphoreType.DMA
    row = (16, PAIR_LEN)
    result = pl.pallas_call(
        kernel,
        out_shape=jax.ShapeDtypeStruct((2, *row), F32),
        in_specs=[
            vmem,
            pl.BlockSpec(memory_space=pl.ANY),
            vmem,
            pl.BlockSpec(memory_space=pltpu.SMEM),
            vmem,
            vmem,
            vmem,
        ],
        out_specs=vmem,
        scratch_shapes=[
            pltpu.VMEM((64, 32, PAIR_LEN), F32),
            pltpu.VMEM((32, 192, PAIR_LEN), BF16),
            pltpu.VMEM((2, 16, 32, 256), F32),
            pltpu.VMEM((512, 512), BF16),
            pltpu.VMEM((512, 512), BF16),
            pltpu.VMEM((512, 128), BF16),
            pltpu.VMEM((512, 128), BF16),
            pltpu.VMEM((512, 128), F32),
            pltpu.VMEM((2, 256, 512), BF16),
            pltpu.VMEM((2, 2, 256, 128), F32),
            pltpu.VMEM((2, 2, 256, 128), F32),
            pltpu.VMEM((16, 64, 256), BF16),
            pltpu.VMEM((2, 2, 8, *row), F32),
            pltpu.VMEM((2, 8, *row), F32),
            pltpu.VMEM((2, 2, *row), F32),
            pltpu.VMEM((2, 2, *row), F32),
            pltpu.VMEM((2, 2, *row), F32),
            pltpu.VMEM((2, 2, *row), F32),
            pltpu.VMEM((2, 2, *row), F32),
            pltpu.VMEM((2, *row), F32),
            dma((4,)),
            dma((2, 15)), dma((2, 16)),
            dma((2, 2, 15)), dma((2, 2, 16)),
            dma((2,)), dma((2,)),
            dma((2, 4)), dma((2, 4)),
            dma((2, 2)), dma((2, 2)),
            dma((2,)), dma((2,)),
        ],
        compiler_params=pltpu.CompilerParams(
            collective_id=0, has_side_effects=True, vmem_limit_bytes=40 * 1024 * 1024
        ),
        name="harmonics",
    )(
        fields,
        legendre,
        pair_table.reshape(1, -1),
        pair_table,
        jnp.asarray(twiddle),
        jnp.asarray(inner_high),
        jnp.asarray(inner_low),
    )
    return result.reshape(2, 2, 8, PAIR_LEN)


def solution(mesh):
    placed = (P(None, None, "theta", "phi"), P("theta", "phi", None), P())
    return jax.shard_map(
        on_device,
        mesh=mesh,
        in_specs=placed,
        out_specs=P(("phi", "theta"), None, None, None),
        check_vma=False,
    )
```

time: 84 us -> 84 us (level)
  local copies, waits for them, and re-layouts: 1.58 us -> 8.81 us
  Pallas kernels: 80.9 us -> 74.4 us
    unnamed x1 -> x13, local copies, waits for them, and re-layouts: 1.58 us -> 8.81 us
    pallas_call x1, Pallas kernels: 80.9 us -> 74.4 us  [on_device(): pl.pallas_call(kernel, out_shape=jax.ShapeDtypeStruct((2, *row), F32), in...]
where the time goes in v3:
time: 84 us; the launch traced here: 83.2 us
  Pallas kernels  74.4 us (89%)
  local copies, waits for them, and re-layouts  8.81 us (10%)
    pallas_call x1, Pallas kernels, on_device(): pl.pallas_call(kernel, out_shape=jax.ShapeDtypeStruct((2, *row), F32), in...  74.4 us
    unnamed x13, local copies, waits for them, and re-layouts  8.81 us

profile of v3, /device:TPU:1, one launch (start us, length us, event | category | flops | bytes accessed | tf_op | source)
XLA Modules:
  0.0 83.2 jit_solution(10404557105834468662)
XLA Ops:
  0.0 0.0 copy-start
  0.0 3.7 %copy-done = f32[64,32,1025]{2,1,0:T(8,128)S(1)} copy-done((f32[64,32,1025]{2,1,0:T(8,128)S(1)}, f32[64,32,1025]{2,1,0:T(8,128)}, u32[]{:S(2)}) %copy-start) | copy-done | bytes 8396824
  3.7 0.0 copy-start.1
  3.7 1.2 %copy-done.1 = f32[8,2,64,256]{3,2,1,0:T(8,128)S(1)} copy-done((f32[8,2,64,256]{3,2,1,0:T(8,128)S(1)}, f32[8,2,64,256]{3,2,1,0:T(8,128)}, u32[]{:S(2)}) %copy-start.1) | copy-done | bytes 1048600
  4.9 0.0 copy-start.2
  4.9 0.9 %copy-done.2 = bf16[128,512]{1,0:T(8,128)(2,1)S(1)} copy-done((bf16[128,512]{1,0:T(8,128)(2,1)S(1)}, bf16[128,512]{1,0:T(8,128)(2,1)}, u32[]{:S(2)}) %copy-start.2) | copy-done | bytes 131096
  5.8 0.0 copy-start.3
  5.8 0.9 %copy-done.3 = bf16[128,512]{1,0:T(8,128)(2,1)S(1)} copy-done((bf16[128,512]{1,0:T(8,128)(2,1)S(1)}, bf16[128,512]{1,0:T(8,128)(2,1)}, u32[]{:S(2)}) %copy-start.3) | copy-done | bytes 131096
  6.7 0.0 copy-start.4
  6.7 0.8 copy-done.4
  7.5 0.0 copy-start.5
  7.5 0.7 copy-done.5
  8.2 74.4 %harmonics.1 = f32[2,16,1025]{2,1,0:T(8,128)S(1)} custom-call(f32[8,2,64,256]{3,2,1,0:T(8,128)S(1)} %copy-done.1, f32[64,32,1025]{2,1,0:T(8,128)S(1)} %copy-done, s32[1,512]{1,0:T(1,128)S(1)} %bitcast.3, s32[512]{0:T(512)S(1)} %copy-done.5, f32[2,16,256]{2,1,0:T(8,128)S(1)} %copy-done.4, bf16[128,512]{1,0:T(8,128)(2,1)S(1)} %copy-done.3, ...), custom_call_target="tpu_custom_call" | custom-call | tf_op jit(solution)/shard_map/harmonics/pallas_call | solution.py:352
  82.6 0.7 copy.8
Async XLA Ops:
  0.0 3.7 %copy-start = (f32[64,32,1025]{2,1,0:T(8,128)S(1)}, f32[64,32,1025]{2,1,0:T(8,128)}, u32[]{:S(2)}) copy-start(f32[64,32,1025]{2,1,0:T(8,128)} %legendre.1) | copy-start | bytes 25190404
  3.7 1.2 %copy-start.1 = (f32[8,2,64,256]{3,2,1,0:T(8,128)S(1)}, f32[8,2,64,256]{3,2,1,0:T(8,128)}, u32[]{:S(2)}) copy-start(f32[8,2,64,256]{3,2,1,0:T(8,128)} %fields.1) | copy-start | bytes 3145732
  4.9 0.9 %copy-start.2 = (bf16[128,512]{1,0:T(8,128)(2,1)S(1)}, bf16[128,512]{1,0:T(8,128)(2,1)}, u32[]{:S(2)}) copy-start(bf16[128,512]{1,0:T(8,128)(2,1)} %constant.8.clone.inner_low) | copy-start | bytes 393220
  5.8 0.9 %copy-start.3 = (bf16[128,512]{1,0:T(8,128)(2,1)S(1)}, bf16[128,512]{1,0:T(8,128)(2,1)}, u32[]{:S(2)}) copy-start(bf16[128,512]{1,0:T(8,128)(2,1)} %constant.7.clone.inner_high) | copy-start | bytes 393220
  6.7 0.8 copy-start.4
  7.5 0.7 copy-start.5
